TPU v7x, 32 devices: a whole 2x2x4 slice. The times are simulated.
32 devices in a mesh: row: 4 (over y, x), col: 4 (over z), fiber: 2 (over core).
Axes of the slice: x: 2, y: 2, z: 4, core: 2. Of those that a mesh axis runs over, the one named last changes fastest.
Arguments:
- user_factors: float32 [8192, 128], P(('row', 'col', 'fiber')), may hold values from -3 to 3
- item_factors: bfloat16 [16384, 128], P(('row', 'col')), may hold values from -0.119628906 to 0.119628906
- ratings: bfloat16 [4, 4, 256, 128, 128], P('row', 'col', 'fiber'), may hold values from -2 to 2, as said below
- block_user: int32 [4, 4, 256], P('row', 'col', 'fiber'), may hold values from 0 to 15, as said below
- block_item: int32 [4, 4, 256], P('row', 'col', 'fiber'), may hold values from 0 to 31, as said below
- counts: int32 [8192], P(('row', 'col', 'fiber')), may hold values from 1 to 8192, as said below
Outputs:
- factors: float32 [8192, 128], P(('row', 'col', 'fiber'))
- residual: float32 [8192, 128], P(('row', 'col', 'fiber'))
Inputs may be any that keep to these rules, and one draw needn't show every extreme that they name: `block_user`: within one tile (one row index and one column index) the occupied blocks are distinct; each user block index appears in exactly 16 blocks of every tile, which fall on the two fiber halves at random. `block_item`: an item block index within the column slab. counts[u] equals the number of nonzero entries of ratings that belong to user u, over all blocks; some user has every rating of its blocks observed. Every user row of every occupied block has an observed rating; observed ratings have magnitude 0.25 or more.
All inputs are finite; a program needn't handle non-finite values.
Results may differ from a plain program's by a relative error of at most 0.012.
The roundings to bfloat16 on the way count: a program that leaves them out, or rounds other values in their place, can miss the bound.
Values may be sent and summed in bfloat16 or wider, within the bound.
A program may use at most 64 MiB of HBM per device.

v0:
```python
import jax
import jax.numpy as jnp
from jax import lax
from jax.sharding import PartitionSpec as P

ITERS = 2


reg_weight = 0.0004
tiny = 1e-06


def block_terms(slab_values, item_slab, rating_blocks, owners, columns, with_ratings):
    block_count = rating_blocks.shape[0]
    block_size = rating_blocks.shape[1]
    factor_rank = slab_values.shape[1]
    user_count = slab_values.shape[0] // block_size
    user_table = slab_values.reshape(user_count, block_size, factor_rank)
    item_table = item_slab.reshape(item_slab.shape[0] // block_size, block_size, factor_rank)
    group_size = 32

    def visit(running, pieces):
        rating_block, group_owners, group_columns = pieces
        user_rows = user_table[group_owners]
        item_rows = item_table[group_columns]
        predicted = jnp.einsum(
            "nik,njk->nij", user_rows, item_rows, preferred_element_type=jnp.float32
        )
        observed = (rating_block != 0).astype(jnp.float32)
        if with_ratings:
            weights = (rating_block.astype(jnp.float32) - observed * predicted).astype(jnp.bfloat16)
        else:
            weights = (observed * predicted).astype(jnp.bfloat16)
        contribution = jnp.einsum(
            "nij,njk->nik", weights, item_rows, preferred_element_type=jnp.float32
        )
        return (running.at[group_owners].add(contribution), None)

    groups = block_count // group_size
    pieces = (
        rating_blocks.reshape(groups, group_size, block_size, block_size),
        owners.reshape(groups, group_size),
        columns.reshape(groups, group_size),
    )
    initial = jnp.zeros((user_count, block_size, factor_rank), jnp.float32)
    running, unused = lax.scan(visit, initial, pieces)
    return running.reshape(user_count * block_size, factor_rank)


def per_device(user_factors, item_factors, ratings, block_user, block_item, counts):
    item_slab = lax.all_gather(item_factors, "row", axis=0, tiled=True)
    rating_blocks = ratings[0, 0]
    owners = block_user[0, 0]
    columns = block_item[0, 0]
    damping = reg_weight * counts.astype(jnp.float32)[:, None]
    slab_start = lax.all_gather(
        user_factors.astype(jnp.bfloat16), ("col", "fiber"), axis=0, tiled=True
    )
    initial_terms = block_terms(slab_start, item_slab, rating_blocks, owners, columns, True)
    factors = user_factors
    residual = (
        lax.psum_scatter(initial_terms, ("col", "fiber"), scatter_dimension=0, tiled=True)
        - damping * factors
    )
    direction = residual
    squares = jnp.sum(residual * residual, axis=1, keepdims=True)
    for iteration in range(ITERS):
        slab_direction = lax.all_gather(
            direction.astype(jnp.bfloat16), ("col", "fiber"), axis=0, tiled=True
        )
        partial_value = block_terms(
            slab_direction, item_slab, rating_blocks, owners, columns, False
        )
        image = (
            lax.psum_scatter(partial_value, ("col", "fiber"), scatter_dimension=0, tiled=True)
            + damping * direction
        )
        step_size = squares / (jnp.sum(direction * image, axis=1, keepdims=True) + tiny)
        factors = factors + step_size * direction
        residual = residual - step_size * image
        if iteration + 1 < ITERS:
            renewed = jnp.sum(residual * residual, axis=1, keepdims=True)
            direction = residual + renewed / (squares + tiny) * direction
            squares = renewed
    return (factors, residual)


def solution(mesh):
    return jax.shard_map(
        per_device,
        mesh=mesh,
        in_specs=(
            P(("row", "col", "fiber"), None),
            P(("row", "col"), None),
            P("row", "col", "fiber", None, None),
            P("row", "col", "fiber"),
            P("row", "col", "fiber"),
            P(("row", "col", "fiber")),
        ),
        out_specs=(P(("row", "col", "fiber"), None), P(("row", "col", "fiber"), None)),
        check_vma=False,
    )
```

profile of v0, /device:TPU:0, one launch (start us, length us, event | category | flops | bytes accessed | tf_op | source)
XLA Modules:
  0.0 321.2 jit_solution(1297319421898585079)
XLA Ops:
  9.9 1.3 reduce.7
  12.2 17.5 %all_gather.12 = bf16[2048,128]{1,0:T(8,128)(2,1)} all-gather(bf16[256,128]{1,0:T(8,128)(2,1)S(1)} %convert_element_type.30), channel_id=1, replica_groups=mesh['row'=4,'col'=4,'fiber'=2] {'col','fiber'}, dimensions={0}, use_global_device_ids=true | all-gather | bytes 589824 | tf_op jit(solution)/shard_map/all_gather | solution.py:56
  29.7 9.4 %all-gather.2.cloned.1.call-done = bf16[4096,128]{1,0:T(8,128)(2,1)} async-done(((bf16[1024,128]{1,0:T(8,128)(2,1)}), bf16[4096,128]{1,0:T(8,128)(2,1)}) %all-gather.2.cloned.1.call-update) | async-done | bytes 1048592 | tf_op jit(solution)/shard_map/all_gather | solution.py:51
  40.2 49.7 %while.30 = (s32[]{:T(128)}, f32[16,128,128]{2,1,0:T(8,128)}, s32[4,32]{1,0:T(4,128)S(1)}, bf16[4,32,128,128]{3,2,1,0:T(8,128)(2,1)}, bf16[16,128,128]{2,1,0:T(8...) while((s32[]{:T(128)}, f32[16,128,128]{2,1,0:T(8,128)}, ...), condition=%wide.region_2.3_spmd, body=%wide.region_0.2_spmd.sunk | while | flops 271583424 | bytes 20981492 | solution.py:46
  40.2 2.8 gather_fusion.1
  43.8 2.7 fusion.65
  46.5 6.1 %scatter_fusion = f32[16,128,128]{2,1,0:T(8,128)} fusion(f32[16,128,128]{2,1,0:T(8,128)} %get-tuple-element.320, s32[32]{0:T(128)S(1)} %get-tuple-element.291, f32[32,128,128]{2,1,0:T(8,128)S(1)} %fusion.65), kind=kCustom, calls=%fused_computation.6.clone.1 | custom fusion | flops 524288 | bytes 6291584 | tf_op jit(solution)/shard_map/while/body/eval_jaxpr/scatter-add | solution.py:37
  52.6 2.8 gather_fusion.1
  56.2 2.7 fusion.65
  58.9 6.2 %scatter_fusion = f32[16,128,128]{2,1,0:T(8,128)} fusion(f32[16,128,128]{2,1,0:T(8,128)} %get-tuple-element.320, s32[32]{0:T(128)S(1)} %get-tuple-element.291, f32[32,128,128]{2,1,0:T(8,128)S(1)} %fusion.65), kind=kCustom, calls=%fused_computation.6.clone.1 | custom fusion | flops 524288 | bytes 6291584 | tf_op jit(solution)/shard_map/while/body/eval_jaxpr/scatter-add | solution.py:37
  65.1 2.8 gather_fusion.1
  68.7 2.7 fusion.65
  71.4 6.1 %scatter_fusion = f32[16,128,128]{2,1,0:T(8,128)} fusion(f32[16,128,128]{2,1,0:T(8,128)} %get-tuple-element.320, s32[32]{0:T(128)S(1)} %get-tuple-element.291, f32[32,128,128]{2,1,0:T(8,128)S(1)} %fusion.65), kind=kCustom, calls=%fused_computation.6.clone.1 | custom fusion | flops 524288 | bytes 6291584 | tf_op jit(solution)/shard_map/while/body/eval_jaxpr/scatter-add | solution.py:37
  77.5 2.8 gather_fusion.1
  81.1 2.7 fusion.65
  83.8 6.1 %scatter_fusion = f32[16,128,128]{2,1,0:T(8,128)} fusion(f32[16,128,128]{2,1,0:T(8,128)} %get-tuple-element.320, s32[32]{0:T(128)S(1)} %get-tuple-element.291, f32[32,128,128]{2,1,0:T(8,128)S(1)} %fusion.65), kind=kCustom, calls=%fused_computation.6.clone.1 | custom fusion | flops 524288 | bytes 6291584 | tf_op jit(solution)/shard_map/while/body/eval_jaxpr/scatter-add | solution.py:37
  90.0 32.6 %reduce-scatter.4.cloned.1.call-done = f32[256,128]{1,0:T(8,128)} async-done(((f32[2048,128]{1,0:T(8,128)}), f32[256,128]{1,0:T(8,128)}) %reduce-scatter.4.cloned.1.call-update) | async-done | bytes 131088 | tf_op jit(solution)/shard_map/reduce_scatter | solution.py:62
  123.6 14.9 %all_gather.14 = bf16[2048,128]{1,0:T(8,128)(2,1)S(1)} all-gather(bf16[256,128]{1,0:T(8,128)(2,1)S(1)} %get-tuple-element.160), channel_id=1, replica_groups=mesh['row'=4,'col'=4,'fiber'=2] {'col','fiber'}, dimensions={0}, use_global_device_ids=true | all-gather | bytes 589824 | tf_op jit(solution)/shard_map/all_gather | solution.py:68
  138.7 44.9 %while.31 = (s32[]{:T(128)}, f32[16,128,128]{2,1,0:T(8,128)S(1)}, s32[4,32]{1,0:T(4,128)S(1)}, bf16[4,32,128,128]{3,2,1,0:T(8,128)(2,1)}, bf16[16,128,128]{2,1,0...) while((s32[]{:T(128)}, f32[16,128,128]{2,1,0:T(8,128)S(1)}, ...), condition=%wide.region_7.8_spmd, body=%wide.region_5.7_spmd.sunk | while | flops 270534848 | bytes 20981520 | solution.py:46
  138.7 1.7 gather_fusion.3
  141.2 4.0 %fusion.70 = f32[32,128,128]{2,1,0:T(8,128)} fusion(bf16[32,128,128]{2,1,0:T(8,128)(2,1)S(1)} %gather_fusion.2, bf16[32,128,128]{2,1,0:T(8,128)(2,1)} %gather_fusion.3, bf16[4,32,128,128]{3,2,1,0:T(8,128)(2,1)} %get-tuple-element.354, s32[]{:T(128)} %get-tuple-element.343), kind=kOutput, calls=%fused_computation.30.clone.1 | convolution fusion | flops 270008320 | bytes 6291968 | tf_op jit(solution)/shard_map/while/body/eval_jaxpr/nij,njk->nik/dot_general | solution.py:34
  145.2 4.7 %scatter_fusion.1 = f32[16,128,128]{2,1,0:T(8,128)S(1)} fusion(f32[16,128,128]{2,1,0:T(8,128)S(1)} %get-tuple-element.344, s32[32]{0:T(128)S(1)} %get-tuple-element.300, f32[32,128,128]{2,1,0:T(8,128)} %fusion.70), kind=kCustom, calls=%fused_computation.7.clone.1 | custom fusion | flops 524288 | bytes 6291584 | tf_op jit(solution)/shard_map/while/body/eval_jaxpr/scatter-add | solution.py:37
  149.9 1.7 gather_fusion.3
  152.4 4.0 %fusion.70 = f32[32,128,128]{2,1,0:T(8,128)} fusion(bf16[32,128,128]{2,1,0:T(8,128)(2,1)S(1)} %gather_fusion.2, bf16[32,128,128]{2,1,0:T(8,128)(2,1)} %gather_fusion.3, bf16[4,32,128,128]{3,2,1,0:T(8,128)(2,1)} %get-tuple-element.354, s32[]{:T(128)} %get-tuple-element.343), kind=kOutput, calls=%fused_computation.30.clone.1 | convolution fusion | flops 270008320 | bytes 6291968 | tf_op jit(solution)/shard_map/while/body/eval_jaxpr/nij,njk->nik/dot_general | solution.py:34
  156.4 4.7 %scatter_fusion.1 = f32[16,128,128]{2,1,0:T(8,128)S(1)} fusion(f32[16,128,128]{2,1,0:T(8,128)S(1)} %get-tuple-element.344, s32[32]{0:T(128)S(1)} %get-tuple-element.300, f32[32,128,128]{2,1,0:T(8,128)} %fusion.70), kind=kCustom, calls=%fused_computation.7.clone.1 | custom fusion | flops 524288 | bytes 6291584 | tf_op jit(solution)/shard_map/while/body/eval_jaxpr/scatter-add | solution.py:37
  161.2 1.7 gather_fusion.3
  163.6 4.0 %fusion.70 = f32[32,128,128]{2,1,0:T(8,128)} fusion(bf16[32,128,128]{2,1,0:T(8,128)(2,1)S(1)} %gather_fusion.2, bf16[32,128,128]{2,1,0:T(8,128)(2,1)} %gather_fusion.3, bf16[4,32,128,128]{3,2,1,0:T(8,128)(2,1)} %get-tuple-element.354, s32[]{:T(128)} %get-tuple-element.343), kind=kOutput, calls=%fused_computation.30.clone.1 | convolution fusion | flops 270008320 | bytes 6291968 | tf_op jit(solution)/shard_map/while/body/eval_jaxpr/nij,njk->nik/dot_general | solution.py:34
  167.6 4.7 %scatter_fusion.1 = f32[16,128,128]{2,1,0:T(8,128)S(1)} fusion(f32[16,128,128]{2,1,0:T(8,128)S(1)} %get-tuple-element.344, s32[32]{0:T(128)S(1)} %get-tuple-element.300, f32[32,128,128]{2,1,0:T(8,128)} %fusion.70), kind=kCustom, calls=%fused_computation.7.clone.1 | custom fusion | flops 524288 | bytes 6291584 | tf_op jit(solution)/shard_map/while/body/eval_jaxpr/scatter-add | solution.py:37
  172.4 1.7 gather_fusion.3
  174.8 4.0 %fusion.70 = f32[32,128,128]{2,1,0:T(8,128)} fusion(bf16[32,128,128]{2,1,0:T(8,128)(2,1)S(1)} %gather_fusion.2, bf16[32,128,128]{2,1,0:T(8,128)(2,1)} %gather_fusion.3, bf16[4,32,128,128]{3,2,1,0:T(8,128)(2,1)} %get-tuple-element.354, s32[]{:T(128)} %get-tuple-element.343), kind=kOutput, calls=%fused_computation.30.clone.1 | convolution fusion | flops 270008320 | bytes 6291968 | tf_op jit(solution)/shard_map/while/body/eval_jaxpr/nij,njk->nik/dot_general | solution.py:34
  178.9 4.7 %scatter_fusion.1 = f32[16,128,128]{2,1,0:T(8,128)S(1)} fusion(f32[16,128,128]{2,1,0:T(8,128)S(1)} %get-tuple-element.344, s32[32]{0:T(128)S(1)} %get-tuple-element.300, f32[32,128,128]{2,1,0:T(8,128)} %fusion.70), kind=kCustom, calls=%fused_computation.7.clone.1 | custom fusion | flops 524288 | bytes 6291584 | tf_op jit(solution)/shard_map/while/body/eval_jaxpr/scatter-add | solution.py:37
  184.6 31.0 %reduce-scatter.6.cloned.1.call-done = f32[256,128]{1,0:T(8,128)} async-done(((f32[2048,128]{1,0:T(8,128)}), f32[256,128]{1,0:T(8,128)}) %reduce-scatter.6.cloned.1.call-update) | async-done | bytes 131088 | tf_op jit(solution)/shard_map/reduce_scatter | solution.py:75
  219.0 14.9 %all_gather.15 = bf16[2048,128]{1,0:T(8,128)(2,1)S(1)} all-gather(bf16[256,128]{1,0:T(8,128)(2,1)S(1)} %fusion.35), channel_id=1, replica_groups=mesh['row'=4,'col'=4,'fiber'=2] {'col','fiber'}, dimensions={0}, use_global_device_ids=true | all-gather | bytes 589824 | tf_op jit(solution)/shard_map/all_gather | solution.py:68
  234.1 45.0 %while.32 = (s32[]{:T(128)}, f32[16,128,128]{2,1,0:T(8,128)S(1)}, s32[4,32]{1,0:T(4,128)S(1)}, bf16[4,32,128,128]{3,2,1,0:T(8,128)(2,1)}, bf16[16,128,128]{2,1,0...) while((s32[]{:T(128)}, f32[16,128,128]{2,1,0:T(8,128)S(1)}, ...), condition=%wide.region_13.14_spmd, body=%wide.region_11.13_spmd.sunk | while | flops 270534848 | bytes 20985672 | solution.py:46
  234.1 1.7 gather_fusion.5
  236.6 4.0 %fusion.75 = f32[32,128,128]{2,1,0:T(8,128)} fusion(bf16[32,128,128]{2,1,0:T(8,128)(2,1)S(1)} %gather_fusion.4, bf16[32,128,128]{2,1,0:T(8,128)(2,1)} %gather_fusion.5, bf16[4,32,128,128]{3,2,1,0:T(8,128)(2,1)} %get-tuple-element.378, s32[]{:T(128)} %get-tuple-element.367), kind=kOutput, calls=%fused_computation.48.clone.1 | convolution fusion | flops 270008320 | bytes 6291968 | tf_op jit(solution)/shard_map/while/body/eval_jaxpr/nij,njk->nik/dot_general | solution.py:34
  240.6 4.7 %scatter_fusion.2 = f32[16,128,128]{2,1,0:T(8,128)S(1)} fusion(f32[16,128,128]{2,1,0:T(8,128)S(1)} %get-tuple-element.368, s32[32]{0:T(128)S(1)} %get-tuple-element.309, f32[32,128,128]{2,1,0:T(8,128)} %fusion.75), kind=kCustom, calls=%fused_computation.8.clone.1 | custom fusion | flops 524288 | bytes 6291584 | tf_op jit(solution)/shard_map/while/body/eval_jaxpr/scatter-add | solution.py:37
  245.4 1.7 gather_fusion.5
  247.8 4.0 %fusion.75 = f32[32,128,128]{2,1,0:T(8,128)} fusion(bf16[32,128,128]{2,1,0:T(8,128)(2,1)S(1)} %gather_fusion.4, bf16[32,128,128]{2,1,0:T(8,128)(2,1)} %gather_fusion.5, bf16[4,32,128,128]{3,2,1,0:T(8,128)(2,1)} %get-tuple-element.378, s32[]{:T(128)} %get-tuple-element.367), kind=kOutput, calls=%fused_computation.48.clone.1 | convolution fusion | flops 270008320 | bytes 6291968 | tf_op jit(solution)/shard_map/while/body/eval_jaxpr/nij,njk->nik/dot_general | solution.py:34
  251.9 4.7 %scatter_fusion.2 = f32[16,128,128]{2,1,0:T(8,128)S(1)} fusion(f32[16,128,128]{2,1,0:T(8,128)S(1)} %get-tuple-element.368, s32[32]{0:T(128)S(1)} %get-tuple-element.309, f32[32,128,128]{2,1,0:T(8,128)} %fusion.75), kind=kCustom, calls=%fused_computation.8.clone.1 | custom fusion | flops 524288 | bytes 6291584 | tf_op jit(solution)/shard_map/while/body/eval_jaxpr/scatter-add | solution.py:37
  256.6 1.7 gather_fusion.5
  259.1 4.0 %fusion.75 = f32[32,128,128]{2,1,0:T(8,128)} fusion(bf16[32,128,128]{2,1,0:T(8,128)(2,1)S(1)} %gather_fusion.4, bf16[32,128,128]{2,1,0:T(8,128)(2,1)} %gather_fusion.5, bf16[4,32,128,128]{3,2,1,0:T(8,128)(2,1)} %get-tuple-element.378, s32[]{:T(128)} %get-tuple-element.367), kind=kOutput, calls=%fused_computation.48.clone.1 | convolution fusion | flops 270008320 | bytes 6291968 | tf_op jit(solution)/shard_map/while/body/eval_jaxpr/nij,njk->nik/dot_general | solution.py:34
  263.1 4.7 %scatter_fusion.2 = f32[16,128,128]{2,1,0:T(8,128)S(1)} fusion(f32[16,128,128]{2,1,0:T(8,128)S(1)} %get-tuple-element.368, s32[32]{0:T(128)S(1)} %get-tuple-element.309, f32[32,128,128]{2,1,0:T(8,128)} %fusion.75), kind=kCustom, calls=%fused_computation.8.clone.1 | custom fusion | flops 524288 | bytes 6291584 | tf_op jit(solution)/shard_map/while/body/eval_jaxpr/scatter-add | solution.py:37
  267.9 1.7 gather_fusion.5
  270.3 4.0 %fusion.75 = f32[32,128,128]{2,1,0:T(8,128)} fusion(bf16[32,128,128]{2,1,0:T(8,128)(2,1)S(1)} %gather_fusion.4, bf16[32,128,128]{2,1,0:T(8,128)(2,1)} %gather_fusion.5, bf16[4,32,128,128]{3,2,1,0:T(8,128)(2,1)} %get-tuple-element.378, s32[]{:T(128)} %get-tuple-element.367), kind=kOutput, calls=%fused_computation.48.clone.1 | convolution fusion | flops 270008320 | bytes 6291968 | tf_op jit(solution)/shard_map/while/body/eval_jaxpr/nij,njk->nik/dot_general | solution.py:34
  274.4 4.7 %scatter_fusion.2 = f32[16,128,128]{2,1,0:T(8,128)S(1)} fusion(f32[16,128,128]{2,1,0:T(8,128)S(1)} %get-tuple-element.368, s32[32]{0:T(128)S(1)} %get-tuple-element.309, f32[32,128,128]{2,1,0:T(8,128)} %fusion.75), kind=kCustom, calls=%fused_computation.8.clone.1 | custom fusion | flops 524288 | bytes 6291584 | tf_op jit(solution)/shard_map/while/body/eval_jaxpr/scatter-add | solution.py:37
  280.1 30.9 %reduce-scatter.8.cloned.1.call-done = f32[256,128]{1,0:T(8,128)} async-done(((f32[2048,128]{1,0:T(8,128)}), f32[256,128]{1,0:T(8,128)}) %reduce-scatter.8.cloned.1.call-update) | async-done | bytes 131088 | tf_op jit(solution)/shard_map/reduce_scatter | solution.py:75
  312.9 1.8 multiply_subtract_fusion
  (147 shorter events, 22.6 us)
Async XLA Ops:
  7.2 31.9 %all-gather.2.cloned.1.call-start = ((), (), s32[]{:S(2)}) async-start(), calls=%async_computation.3 | async-start | bytes 1310720 | tf_op jit(solution)/shard_map/all_gather | solution.py:51
  7.9 114.7 %reduce-scatter.4.cloned.1.call-start = ((), (), s32[]{:S(2)}) async-start(), calls=%async_computation.4 | async-start | bytes 1179648 | tf_op jit(solution)/shard_map/reduce_scatter | solution.py:62
  40.2 49.7 %copy-start.15 = (s32[256]{0:T(256)S(1)}, s32[256]{0:T(256)}, u32[]{:S(2)}) copy-start(s32[256]{0:T(256)} %param.17) | copy-start | bytes 3076
  40.2 82.4 %copy-start.9 = (f32[256,128]{1,0:T(8,128)S(1)}, f32[256,128]{1,0:T(8,128)}, u32[]{:S(2)}) copy-start(f32[256,128]{1,0:T(8,128)} %param.12) | copy-start | bytes 393220
  40.2 2.8 copy-start
  52.6 2.8 copy-start
  65.1 2.8 copy-start
  77.5 2.8 copy-start
  89.9 48.8 %copy-start.1 = (bf16[32,128,128]{2,1,0:T(8,128)(2,1)S(1)}, bf16[32,128,128]{2,1,0:T(8,128)(2,1)}, u32[]{:S(2)}) copy-start(bf16[32,128,128]{2,1,0:T(8,128)(2,1)} %get-tuple-element.388) | copy-start | bytes 3145732
  89.9 125.7 %reduce-scatter.6.cloned.1.call-start = ((), (), s32[]{:S(2)}) async-start(), calls=%async_computation.5 | async-start | bytes 1179648 | tf_op jit(solution)/shard_map/reduce_scatter | solution.py:75
  138.7 1.7 copy-start.6
  145.2 4.7 %copy-start.7 = (bf16[16,128,128]{2,1,0:T(8,128)(2,1)S(1)}, bf16[16,128,128]{2,1,0:T(8,128)(2,1)}, u32[]{:S(2)}) copy-start(bf16[16,128,128]{2,1,0:T(8,128)(2,1)} %copy-done.6) | copy-start | bytes 1572868 | tf_op jit(solution)/shard_map/while
  149.9 1.7 copy-start.6
  156.4 4.7 %copy-start.7 = (bf16[16,128,128]{2,1,0:T(8,128)(2,1)S(1)}, bf16[16,128,128]{2,1,0:T(8,128)(2,1)}, u32[]{:S(2)}) copy-start(bf16[16,128,128]{2,1,0:T(8,128)(2,1)} %copy-done.6) | copy-start | bytes 1572868 | tf_op jit(solution)/shard_map/while
  161.1 1.7 copy-start.6
  167.6 4.7 %copy-start.7 = (bf16[16,128,128]{2,1,0:T(8,128)(2,1)S(1)}, bf16[16,128,128]{2,1,0:T(8,128)(2,1)}, u32[]{:S(2)}) copy-start(bf16[16,128,128]{2,1,0:T(8,128)(2,1)} %copy-done.6) | copy-start | bytes 1572868 | tf_op jit(solution)/shard_map/while
  172.3 1.7 copy-start.6
  178.9 4.7 %copy-start.7 = (bf16[16,128,128]{2,1,0:T(8,128)(2,1)S(1)}, bf16[16,128,128]{2,1,0:T(8,128)(2,1)}, u32[]{:S(2)}) copy-start(bf16[16,128,128]{2,1,0:T(8,128)(2,1)} %copy-done.6) | copy-start | bytes 1572868 | tf_op jit(solution)/shard_map/while
  183.5 1.0 copy-start.3
  184.5 126.5 %reduce-scatter.8.cloned.1.call-start = ((), (), s32[]{:S(2)}) async-start(), calls=%async_computation.6 | async-start | bytes 1179648 | tf_op jit(solution)/shard_map/reduce_scatter | solution.py:75
  216.7 17.3 %copy-start.12 = (f32[256]{0:T(256)}, f32[256]{0:T(256)S(1)}, u32[]{:S(2)}) copy-start(f32[256]{0:T(256)S(1)} %add_divide_fusion.2) | copy-start | bytes 3076
  217.9 16.2 %copy-start.14 = (f32[256]{0:T(256)}, f32[256]{0:T(256)S(1)}, u32[]{:S(2)}) copy-start(f32[256]{0:T(256)S(1)} %multiply_reduce_fusion.1) | copy-start | bytes 3076
  217.9 16.1 %copy-start.13 = (f32[256]{0:T(256)}, f32[256]{0:T(256)S(1)}, u32[]{:S(2)}) copy-start(f32[256]{0:T(256)S(1)} %add_divide_fusion.1) | copy-start | bytes 3076
  234.0 77.0 %copy-start.8 = (f32[256,128]{1,0:T(8,128)S(1)}, f32[256,128]{1,0:T(8,128)}, u32[]{:S(2)}) copy-start(f32[256,128]{1,0:T(8,128)} %reduce-scatter.6.cloned.1.call-done) | copy-start | bytes 393220
  234.1 1.7 copy-start.10
  234.1 1.7 copy-start.4
  240.6 4.7 %copy-start.5 = (bf16[16,128,128]{2,1,0:T(8,128)(2,1)S(1)}, bf16[16,128,128]{2,1,0:T(8,128)(2,1)}, u32[]{:S(2)}) copy-start(bf16[16,128,128]{2,1,0:T(8,128)(2,1)} %copy-done.4) | copy-start | bytes 1572868 | tf_op jit(solution)/shard_map/while
  240.6 4.7 %copy-start.11 = (s32[4,32]{1,0:T(4,128)S(1)}, s32[4,32]{1,0:T(4,128)}, u32[]{:S(2)}) copy-start(s32[4,32]{1,0:T(4,128)} %copy-done.10) | copy-start | bytes 1540 | tf_op jit(solution)/shard_map/while
  245.3 1.7 copy-start.10
  245.3 1.7 copy-start.4
  251.9 4.7 %copy-start.5 = (bf16[16,128,128]{2,1,0:T(8,128)(2,1)S(1)}, bf16[16,128,128]{2,1,0:T(8,128)(2,1)}, u32[]{:S(2)}) copy-start(bf16[16,128,128]{2,1,0:T(8,128)(2,1)} %copy-done.4) | copy-start | bytes 1572868 | tf_op jit(solution)/shard_map/while
  251.9 4.7 %copy-start.11 = (s32[4,32]{1,0:T(4,128)S(1)}, s32[4,32]{1,0:T(4,128)}, u32[]{:S(2)}) copy-start(s32[4,32]{1,0:T(4,128)} %copy-done.10) | copy-start | bytes 1540 | tf_op jit(solution)/shard_map/while
  256.6 1.7 copy-start.10
  256.6 1.7 copy-start.4
  263.1 4.7 %copy-start.5 = (bf16[16,128,128]{2,1,0:T(8,128)(2,1)S(1)}, bf16[16,128,128]{2,1,0:T(8,128)(2,1)}, u32[]{:S(2)}) copy-start(bf16[16,128,128]{2,1,0:T(8,128)(2,1)} %copy-done.4) | copy-start | bytes 1572868 | tf_op jit(solution)/shard_map/while
  263.1 4.7 %copy-start.11 = (s32[4,32]{1,0:T(4,128)S(1)}, s32[4,32]{1,0:T(4,128)}, u32[]{:S(2)}) copy-start(s32[4,32]{1,0:T(4,128)} %copy-done.10) | copy-start | bytes 1540 | tf_op jit(solution)/shard_map/while
  267.8 1.7 copy-start.10
  267.8 1.7 copy-start.4
  274.4 4.7 %copy-start.5 = (bf16[16,128,128]{2,1,0:T(8,128)(2,1)S(1)}, bf16[16,128,128]{2,1,0:T(8,128)(2,1)}, u32[]{:S(2)}) copy-start(bf16[16,128,128]{2,1,0:T(8,128)(2,1)} %copy-done.4) | copy-start | bytes 1572868 | tf_op jit(solution)/shard_map/while
  274.4 4.7 %copy-start.11 = (s32[4,32]{1,0:T(4,128)S(1)}, s32[4,32]{1,0:T(4,128)}, u32[]{:S(2)}) copy-start(s32[4,32]{1,0:T(4,128)} %copy-done.10) | copy-start | bytes 1540 | tf_op jit(solution)/shard_map/while
  279.1 1.0 copy-start.2
Sparse Core Ops, SparseCore 0:
  9.8 29.2 all-gather.1
  90.0 32.5 reduce-scatter.3
  184.7 30.8 reduce-scatter.5
  280.2 30.7 reduce-scatter.7
where the time goes:
time: 323 us; the launch traced here: 321 us
  waiting for transfers between devices  105 us (33%)
  other arithmetic  73.6 us (23%)
  blocking collectives  47.4 us (15%)
  matrix products  43.1 us (13%)
  local copies, waits for them, and re-layouts  37.6 us (12%)
  between operations  13.9 us (4%)
    reduce_scatter x2, waiting for transfers between devices, per_device(): lax.psum_scatter(partial_value, ('col', 'fiber'), scatter_dimension=0, ti...  61.9 us
    scatter-add x12, other arithmetic, visit(): return (running.at[group_owners].add(contribution), None)  61.8 us
    dot_general x12, matrix products, visit(): jnp.einsum('nij,njk->nik', weights, item_rows, preferred_element_type=jnp...  43.1 us
    reduce_scatter x1, waiting for transfers between devices, per_device(): lax.psum_scatter(initial_terms, ('col', 'fiber'), scatter_dimension=0, ti...  32.6 us
    all_gather x2, blocking collectives, per_device(): lax.all_gather(direction.astype(jnp.bfloat16), ('col', 'fiber'), axis=0,...  29.9 us
    gather x12, local copies, waits for them, and re-layouts, visit(): user_rows = user_table[group_owners]  24.5 us
    all_gather x1, blocking collectives, per_device(): lax.all_gather(user_factors.astype(jnp.bfloat16), ('col', 'fiber'), axis=...  17.5 us
    all_gather x1, waiting for transfers between devices, per_device(): item_slab = lax.all_gather(item_factors, 'row', axis=0, tiled=True)  9.38 us
  transfers between devices with their start and end apart: 4, of which 4 were waited for; matrix products, arithmetic and copies ran while one was open for 1% of the time, Pallas kernels for 0%

commit v1 on v0

v1 whole, which is shorter than its diff:
```python
import functools

import jax
import jax.numpy as jnp
from jax import lax
from jax.experimental import pallas as pl
from jax.experimental.pallas import tpu as pltpu
from jax.sharding import PartitionSpec as P

ITERS = 2
GROUP = 4

reg_weight = 0.0004
tiny = 1e-06

MESH = pl.DeviceIdType.MESH


def sweep_kernel(
    sizes, pos_ref, item_ref, uf_ref, damp_ref, items_hbm, ratings_hbm, x_ref, r_ref,
    vbuf, rbuf, pbuf, part, recv, p_ref,
    item_sem, rating_sem, v_send, v_recv, d_send, d_recv, t_send, t_recv, g_send, g_recv, s_send, s_recv,
):
    rows, cols, fibers = sizes
    my_row, my_col, my_fiber = lax.axis_index("row"), lax.axis_index("col"), lax.axis_index("fiber")
    held_items = items_hbm.shape[0]
    share = held_items // fibers
    held_blocks, block = ratings_hbm.shape[0], ratings_hbm.shape[1]
    own_users = uf_ref.shape[0] // block
    per_user = pos_ref.shape[0] // (cols * own_users)

    def row_of(d):
        return lax.rem(my_row + d, rows)

    def col_of(d):
        return lax.rem(my_col + d, cols)

    def fiber_of(d):
        return lax.rem(my_fiber + d, fibers)

    own_items = pl.ds(my_row * held_items, held_items)
    item_load = pltpu.make_async_copy(items_hbm, vbuf.at[own_items], item_sem)
    item_load.start()
    own_ratings = pl.ds(my_fiber * held_blocks, held_blocks)
    rating_load = pltpu.make_async_copy(ratings_hbm, rbuf.at[own_ratings], rating_sem)
    rating_load.start()

    barrier = pltpu.get_barrier_semaphore()
    for d in range(1, rows):
        pl.semaphore_signal(barrier, inc=1, device_id={"row": row_of(d)}, device_id_type=MESH)
    for d in range(1, cols):
        pl.semaphore_signal(barrier, inc=1, device_id={"col": col_of(d)}, device_id_type=MESH)
    for d in range(1, fibers):
        pl.semaphore_signal(barrier, inc=1, device_id={"fiber": fiber_of(d)}, device_id_type=MESH)

    pbuf[0, my_col] = uf_ref[...].astype(jnp.bfloat16)
    pl.semaphore_wait(barrier, rows + cols + fibers - 3)

    def gather_copy(stage, d):
        return pltpu.make_async_remote_copy(
            src_ref=pbuf.at[stage, my_col],
            dst_ref=pbuf.at[stage, my_col],
            send_sem=g_send.at[stage, d],
            recv_sem=g_recv.at[stage, d],
            device_id={"col": col_of(d)},
            device_id_type=MESH,
        )

    def scatter_copy(stage, d):
        return pltpu.make_async_remote_copy(
            src_ref=part.at[stage, d],
            dst_ref=recv.at[stage, d],
            send_sem=s_send.at[stage, d],
            recv_sem=s_recv.at[stage, d],
            device_id={"col": col_of(d)},
            device_id_type=MESH,
        )

    item_sends = []
    for d in range(1, rows):
        copy = pltpu.make_async_remote_copy(
            src_ref=items_hbm.at[pl.ds(my_fiber * share, share)],
            dst_ref=vbuf.at[pl.ds(my_row * held_items + my_fiber * share, share)],
            send_sem=v_send.at[d],
            recv_sem=v_recv.at[d],
            device_id={"row": row_of(d)},
            device_id_type=MESH,
        )
        copy.start()
        item_sends.append(copy)
    for d in range(1, cols):
        gather_copy(0, d).start()
    rating_sends = []
    for e in range(1, fibers):
        copy = pltpu.make_async_remote_copy(
            src_ref=ratings_hbm,
            dst_ref=rbuf.at[own_ratings],
            send_sem=t_send.at[e],
            recv_sem=t_recv.at[e],
            device_id={"fiber": fiber_of(e)},
            device_id_type=MESH,
        )
        copy.start()
        rating_sends.append(copy)
    shared = []
    for d in range(1, rows):
        item_sends[d - 1].wait_recv()
        source = lax.rem(my_row + rows - d, rows)
        piece = pl.ds(source * held_items + my_fiber * share, share)
        for e in range(1, fibers):
            copy = pltpu.make_async_remote_copy(
                src_ref=vbuf.at[piece],
                dst_ref=vbuf.at[piece],
                send_sem=d_send.at[d, e],
                recv_sem=d_recv.at[d, e],
                device_id={"fiber": fiber_of(e)},
                device_id_type=MESH,
            )
            copy.start()
            shared.append(copy)
    item_load.wait()
    rating_load.wait()
    for copy in rating_sends + shared:
        copy.wait_recv()

    def user_terms(stage, col, j):
        rows_of_user = pbuf[stage, col, pl.ds(pl.multiple_of(j * block, block), block), :]
        base = (col * own_users + j) * per_user

        def visit(g, total):
            first = base + g * GROUP
            items = jnp.concatenate([vbuf[item_ref[first + i]] for i in range(GROUP)], axis=0)
            ratings = jnp.concatenate([rbuf[pos_ref[first + i]] for i in range(GROUP)], axis=1)
            predicted = lax.dot_general(
                rows_of_user, items, (((1,), (1,)), ((), ())), preferred_element_type=jnp.float32
            )
            ratings = ratings.astype(jnp.float32)
            if stage == 0:
                weights = jnp.where(ratings != 0, ratings - predicted, 0.0)
            else:
                weights = jnp.where(ratings != 0, predicted, 0.0)
            return total + jnp.dot(
                weights.astype(jnp.bfloat16), items, preferred_element_type=jnp.float32
            )

        return lax.fori_loop(0, per_user // GROUP, visit, jnp.zeros((block, items_hbm.shape[2]), jnp.float32))

    def reduced(stage):
        for d in list(range(1, cols)) + [0]:
            if d:
                pltpu.make_async_remote_copy(
                    src_ref=pbuf.at[stage, my_col],
                    dst_ref=pbuf.at[stage, my_col],
                    send_sem=g_send.at[stage, cols - d],
                    recv_sem=g_recv.at[stage, cols - d],
                    device_id={"col": col_of(cols - d)},
                    device_id_type=MESH,
                ).wait_recv()
            col = col_of(d)

            def one(j, carry):
                part[stage, d, pl.ds(pl.multiple_of(j * block, block), block), :] = user_terms(stage, col, j)
                return carry

            lax.fori_loop(0, own_users, one, 0)
            if d:
                scatter_copy(stage, d).start()
        total = part[stage, 0]
        for d in range(1, cols):
            scatter_copy(stage, d).wait_recv()
            total = total + recv[stage, d]
        return total

    x_ref[...] = uf_ref[...]
    residual = reduced(0) - damp_ref[...] * uf_ref[...]
    r_ref[...] = residual
    p_ref[...] = residual
    squares = jnp.sum(residual * residual, axis=1, keepdims=True)
    for iteration in range(ITERS):
        pbuf[iteration + 1, my_col] = p_ref[...].astype(jnp.bfloat16)
        for d in range(1, cols):
            gather_copy(iteration + 1, d).start()
        image = reduced(iteration + 1) + damp_ref[...] * p_ref[...]
        direction = p_ref[...]
        step_size = squares / (jnp.sum(direction * image, axis=1, keepdims=True) + tiny)
        x_ref[...] = x_ref[...] + step_size * direction
        residual = r_ref[...] - step_size * image
        r_ref[...] = residual
        if iteration + 1 < ITERS:
            renewed = jnp.sum(residual * residual, axis=1, keepdims=True)
            p_ref[...] = residual + renewed / (squares + tiny) * direction
            squares = renewed

    for copy in item_sends + rating_sends + shared:
        copy.wait_send()
    for stage in range(ITERS + 1):
        for d in range(1, cols):
            gather_copy(stage, d).wait_send()
            scatter_copy(stage, d).wait_send()


def per_device(sizes, slab_users, user_factors, item_factors, ratings, block_user, block_item, counts):
    rows, cols, fibers = sizes
    held_blocks, block = ratings.shape[2], ratings.shape[3]
    rank = user_factors.shape[1]
    users = user_factors.shape[0]
    own_users = users // block
    item_blocks = item_factors.shape[0] // block
    per_user = fibers * held_blocks // (slab_users // block)

    both = lax.all_gather(jnp.stack([block_user[0, 0], block_item[0, 0]]), "fiber", axis=0)
    owners = both[:, 0].reshape(-1)
    columns = both[:, 1].reshape(-1)
    here = jnp.arange(owners.shape[0], dtype=jnp.int32)
    keys = owners * owners.shape[0] + here
    ranks = jnp.sum((keys[None, :] < keys[:, None]).astype(jnp.int32), axis=1)
    groups = jnp.arange(cols, dtype=jnp.int32)[:, None] * fibers + lax.axis_index("fiber")
    wanted = (
        groups[:, :, None] * (own_users * per_user)
        + jnp.arange(own_users * per_user, dtype=jnp.int32)[None, None, :]
    ).reshape(-1)
    match = wanted[:, None] == ranks[None, :]
    positions = jnp.sum(jnp.where(match, here[None, :], 0), axis=1)
    items = jnp.sum(jnp.where(match, columns[None, :], 0), axis=1)
    damping = jnp.broadcast_to(reg_weight * counts.astype(jnp.float32)[:, None], (users, rank))

    stages = ITERS + 1
    dma = pltpu.SemaphoreType.DMA
    vmem = pl.BlockSpec(memory_space=pltpu.VMEM)
    smem = pl.BlockSpec(memory_space=pltpu.SMEM)
    hbm = pl.BlockSpec(memory_space=pl.ANY)
    return pl.pallas_call(
        functools.partial(sweep_kernel, sizes),
        out_shape=(
            jax.ShapeDtypeStruct((users, rank), jnp.float32),
            jax.ShapeDtypeStruct((users, rank), jnp.float32),
        ),
        in_specs=[smem, smem, vmem, vmem, hbm, hbm],
        out_specs=(vmem, vmem),
        scratch_shapes=[
            pltpu.VMEM((rows * item_blocks, block, rank), jnp.bfloat16),
            pltpu.VMEM((fibers * held_blocks, block, block), jnp.bfloat16),
            pltpu.VMEM((stages, cols, users, rank), jnp.bfloat16),
            pltpu.VMEM((stages, cols, users, rank), jnp.float32),
            pltpu.VMEM((stages, cols, users, rank), jnp.float32),
            pltpu.VMEM((users, rank), jnp.float32),
            dma,
            dma,
            dma((rows,)),
            dma((rows,)),
            dma((rows, fibers)),
            dma((rows, fibers)),
            dma((fibers,)),
            dma((fibers,)),
            dma((stages, cols)),
            dma((stages, cols)),
            dma((stages, cols)),
            dma((stages, cols)),
        ],
        compiler_params=pltpu.CompilerParams(
            collective_id=0, has_side_effects=True, vmem_limit_bytes=48 * 1024 * 1024
        ),
    )(
        positions,
        items,
        user_factors,
        damping,
        item_factors.reshape(item_blocks, block, rank),
        ratings[0, 0],
    )


def solution(mesh):
    sizes = (mesh.shape["row"], mesh.shape["col"], mesh.shape["fiber"])

    def whole(user_factors, item_factors, ratings, block_user, block_item, counts):
        slab_users = user_factors.shape[0] // sizes[0]
        return jax.shard_map(
            functools.partial(per_device, sizes, slab_users),
            mesh=mesh,
            in_specs=(
                P(("row", "col", "fiber"), None),
                P(("row", "col"), None),
                P("row", "col", "fiber", None, None),
                P("row", "col", "fiber"),
                P("row", "col", "fiber"),
                P(("row", "col", "fiber")),
            ),
            out_specs=(P(("row", "col", "fiber"), None), P(("row", "col", "fiber"), None)),
            check_vma=False,
        )(user_factors, item_factors, ratings, block_user, block_item, counts)

    return whole
```

time: 323 us -> 83.3 us (0.26)
  waiting for transfers between devices: 105 us -> 0 us
  Pallas kernels: 0 us -> 72.7 us
  other arithmetic: 73.6 us -> 1.81 us
  blocking collectives: 47.4 us -> 1.95 us
  matrix products: 43.1 us -> 0 us
  local copies, waits for them, and re-layouts: 37.6 us -> 5.53 us
  between operations: 13.9 us -> 0.67 us
    reduce_scatter x3 -> x0, waiting for transfers between devices: 94.6 us -> none  [the longest x2 61.9 us: per_device(): lax.psum_scatter(partial_value, ('col', 'fiber'), scatter_dimension=0, ti...]
    pallas_call x0 -> x1, Pallas kernels: none -> 72.7 us  [per_device(): pl.pallas_call(functools.partial(sweep_kernel, sizes), out_shape=(jax.Sha...]
    scatter-add x12 -> x0, other arithmetic: 61.8 us -> none  [visit(): return (running.at[group_owners].add(contribution), None)]
    all_gather x3 -> x1, blocking collectives: 47.4 us -> 1.95 us  [per_device(): lax.all_gather(jnp.stack([block_user[0, 0], block_item[0, 0]]), 'fiber',...]
    dot_general x12 -> x0, matrix products: 43.1 us -> none  [visit(): jnp.einsum('nij,njk->nik', weights, item_rows, preferred_element_type=jnp...]
    gather x24 -> x0, local copies, waits for them, and re-layouts: 33.5 us -> none  [the longest x12 24.5 us: visit(): user_rows = user_table[group_owners]]
    all_gather x1 -> x0, waiting for transfers between devices: 9.38 us -> none  [per_device(): item_slab = lax.all_gather(item_factors, 'row', axis=0, tiled=True)]
  transfers between devices with their start and end apart: 4 -> 0, of which waited for: 4 -> 0; matrix products, arithmetic and copies ran while one was open for 1% -> 0% of each run, Pallas kernels for 0% -> 0%
where the time goes in v1:
time: 83.3 us; the launch traced here: 82.7 us
  Pallas kernels  72.7 us (87%)
  local copies, waits for them, and re-layouts  5.53 us (7%)
  blocking collectives  1.95 us (2%)
  other arithmetic  1.81 us (2%)
    pallas_call x1, Pallas kernels, per_device(): pl.pallas_call(functools.partial(sweep_kernel, sizes), out_shape=(jax.Sha...  72.7 us
    unnamed x8, local copies, waits for them, and re-layouts  5.35 us
    all_gather x1, blocking collectives, per_device(): lax.all_gather(jnp.stack([block_user[0, 0], block_item[0, 0]]), 'fiber',...  1.95 us

profile of v1, /device:TPU:0, one launch (start us, length us, event | category | flops | bytes accessed | tf_op | source)
XLA Modules:
  0.0 82.7 jit_solution(15947983713208002108)
XLA Ops:
  0.6 0.7 add_bitcast_fusion
  1.3 1.9 %all-gather.1 = s32[2,2,128]{2,1,0:T(2,128)S(1)} all-gather(s32[1,2,128]{2,1,0:T(2,128)S(1)} %add_bitcast_fusion), channel_id=2, replica_groups=mesh['row'=4,'col'=4,'fiber'=2] {'fiber'}, dimensions={0}, use_global_device_ids=true | all-gather | bytes 3072 | tf_op jit(solution)/shard_map/all_gather | solution.py:211
  3.3 0.2 convert_reduce_fusion
  3.5 0.7 convert_multiply_fusion
  4.2 0.1 iota_add_fusion
  4.2 0.1 add.51
  4.3 0.2 fusion.1
  4.5 0.1 broadcast_in_dim.37.damp_ref
  4.6 0.0 copy-start
  4.6 2.2 %copy-done = bf16[1,1,128,128,128]{4,3,2,1,0:T(8,128)(2,1)S(1)} copy-done((bf16[1,1,128,128,128]{4,3,2,1,0:T(8,128)(2,1)S(1)}, bf16[1,1,128,128,128]{4,3,2,1,0:T(8,128)(2,1)}, u32[]{:S(2)}) %copy-start) | copy-done | bytes 4194328
  6.8 0.0 copy-start.1
  6.8 0.9 %copy-done.1 = bf16[1024,128]{1,0:T(8,128)(2,1)S(1)} copy-done((bf16[1024,128]{1,0:T(8,128)(2,1)S(1)}, bf16[1024,128]{1,0:T(8,128)(2,1)}, u32[]{:S(2)}) %copy-start.1) | copy-done | bytes 262168
  7.7 0.0 copy-start.2
  7.7 0.9 %copy-done.2 = f32[256,128]{1,0:T(8,128)S(1)} copy-done((f32[256,128]{1,0:T(8,128)S(1)}, f32[256,128]{1,0:T(8,128)}, u32[]{:S(2)}) %copy-start.2) | copy-done | bytes 131096
  8.6 72.7 %shard_map.77 = (f32[256,128]{1,0:T(8,128)S(1)}, f32[256,128]{1,0:T(8,128)S(1)}) custom-call(s32[128]{0:T(128)S(1)} %get-tuple-element.3.pos_ref, s32[128]{0:T(128)S(1)} %get-tuple-element.2.item_ref, f32[256,128]{1,0:T(8,128)S(1)} %copy-done.2, f32[256,128]{1,0:T(8,128)S(1)} %broadcast_in_dim.37.damp_ref, bf16[8,128,128]{2,1,0:T(8,128)(2,1)S(1)} %bitcast.11, ...), custom_call_target="tpu_custom_call" | custom-call | tf_op jit(solution)/shard_map/pallas_call | solution.py:232
  81.4 0.7 copy.10
  82.0 0.7 copy.11
  (3 shorter events, 0.0 us)
Async XLA Ops:
  4.6 2.2 %copy-start = (bf16[1,1,128,128,128]{4,3,2,1,0:T(8,128)(2,1)S(1)}, bf16[1,1,128,128,128]{4,3,2,1,0:T(8,128)(2,1)}, u32[]{:S(2)}) copy-start(bf16[1,1,128,128,128]{4,3,2,1,0:T(8,128)(2,1)} %param.8) | copy-start | bytes 12582916
  6.8 0.9 %copy-start.1 = (bf16[1024,128]{1,0:T(8,128)(2,1)S(1)}, bf16[1024,128]{1,0:T(8,128)(2,1)}, u32[]{:S(2)}) copy-start(bf16[1024,128]{1,0:T(8,128)(2,1)} %param.7) | copy-start | bytes 786436
  7.7 0.9 %copy-start.2 = (f32[256,128]{1,0:T(8,128)S(1)}, f32[256,128]{1,0:T(8,128)}, u32[]{:S(2)}) copy-start(f32[256,128]{1,0:T(8,128)} %uf_ref.1) | copy-start | bytes 393220

commit v2 on v1

--- a/solution.py
+++ b/solution.py
@@ -8,7 +8,6 @@
 from jax.sharding import PartitionSpec as P
 
 ITERS = 2
-GROUP = 4
 
 reg_weight = 0.0004
 tiny = 1e-06
@@ -17,27 +16,36 @@
 
 
 def sweep_kernel(
-    sizes, pos_ref, item_ref, uf_ref, damp_ref, items_hbm, ratings_hbm, x_ref, r_ref,
-    vbuf, rbuf, pbuf, part, recv, p_ref,
-    item_sem, rating_sem, v_send, v_recv, d_send, d_recv, t_send, t_recv, g_send, g_recv, s_send, s_recv,
+    sizes, pos_ref, item_ref, uf_hbm, counts_hbm, items_hbm, ratings_hbm, x_ref, r_ref,
+    vbuf, rbuf, pbuf, part, recv, p_ref, damp_ref, counts_ref,
+    user_sem, count_sem, item_sem, rating_sem, v_send, v_recv, d_send, d_recv, t_send, t_recv, g_send, g_recv, s_send, s_recv,
 ):
     rows, cols, fibers = sizes
     my_row, my_col, my_fiber = lax.axis_index("row"), lax.axis_index("col"), lax.axis_index("fiber")
     held_items = items_hbm.shape[0]
     share = held_items // fibers
     held_blocks, block = ratings_hbm.shape[0], ratings_hbm.shape[1]
-    own_users = uf_ref.shape[0] // block
+    own_users = uf_hbm.shape[0] // block
     per_user = pos_ref.shape[0] // (cols * own_users)
 
     def row_of(d):
         return lax.rem(my_row + d, rows)
 
     def col_of(d):
-        return lax.rem(my_col + d, cols)
+        col, bit = my_col, 1
+        while bit <= d:
+            if d & bit:
+                col = col + bit * (1 - 2 * lax.rem(lax.div(my_col, bit), 2))
+            bit *= 2
+        return col
 
     def fiber_of(d):
         return lax.rem(my_fiber + d, fibers)
 
+    user_load = pltpu.make_async_copy(uf_hbm, x_ref, user_sem)
+    user_load.start()
+    count_load = pltpu.make_async_copy(counts_hbm, counts_ref, count_sem)
+    count_load.start()
     own_items = pl.ds(my_row * held_items, held_items)
     item_load = pltpu.make_async_copy(items_hbm, vbuf.at[own_items], item_sem)
     item_load.start()
@@ -53,7 +61,8 @@
     for d in range(1, fibers):
         pl.semaphore_signal(barrier, inc=1, device_id={"fiber": fiber_of(d)}, device_id_type=MESH)
 
-    pbuf[0, my_col] = uf_ref[...].astype(jnp.bfloat16)
+    user_load.wait()
+    pbuf[0, my_col] = x_ref[...].astype(jnp.bfloat16)
     pl.semaphore_wait(barrier, rows + cols + fibers - 3)
 
     def gather_copy(stage, d):
@@ -66,13 +75,13 @@
             device_id_type=MESH,
         )
 
-    def scatter_copy(stage, d):
+    def scatter_copy(stage, d, j):
         return pltpu.make_async_remote_copy(
-            src_ref=part.at[stage, d],
-            dst_ref=recv.at[stage, d],
-            send_sem=s_send.at[stage, d],
-            recv_sem=s_recv.at[stage, d],
-            device_id={"col": col_of(d)},
+            src_ref=part.at[stage, d, j],
+            dst_ref=recv.at[stage, d, j],
+            send_sem=s_send.at[stage, d, j],
+            recv_sem=s_recv.at[stage, d, j],
+            device_id={"col": col_of(d & -d)},
             device_id_type=MESH,
         )
 
@@ -88,7 +97,8 @@
         )
         copy.start()
         item_sends.append(copy)
-    for d in range(1, cols):
+    order = sorted(range(1, cols), key=lambda d: (d & -d, -d))
+    for d in order:
         gather_copy(0, d).start()
     rating_sends = []
     for e in range(1, fibers):
@@ -118,6 +128,13 @@
             )
             copy.start()
             shared.append(copy)
+    count_load.wait()
+    for j in range(own_users):
+        scaled = reg_weight * counts_ref[pl.ds(j, 1), :].astype(jnp.float32)
+        across = jnp.broadcast_to(scaled, (block, block))
+        damp_ref[pl.ds(j * block, block), :] = jnp.broadcast_to(
+            jnp.transpose(across)[:, :1], (block, damp_ref.shape[1])
+        )
     item_load.wait()
     rating_load.wait()
     for copy in rating_sends + shared:
@@ -127,58 +144,55 @@
         rows_of_user = pbuf[stage, col, pl.ds(pl.multiple_of(j * block, block), block), :]
         base = (col * own_users + j) * per_user
 
-        def visit(g, total):
-            first = base + g * GROUP
-            items = jnp.concatenate([vbuf[item_ref[first + i]] for i in range(GROUP)], axis=0)
-            ratings = jnp.concatenate([rbuf[pos_ref[first + i]] for i in range(GROUP)], axis=1)
-            predicted = lax.dot_general(
-                rows_of_user, items, (((1,), (1,)), ((), ())), preferred_element_type=jnp.float32
-            )
-            ratings = ratings.astype(jnp.float32)
-            if stage == 0:
-                weights = jnp.where(ratings != 0, ratings - predicted, 0.0)
-            else:
-                weights = jnp.where(ratings != 0, predicted, 0.0)
-            return total + jnp.dot(
-                weights.astype(jnp.bfloat16), items, preferred_element_type=jnp.float32
-            )
-
-        return lax.fori_loop(0, per_user // GROUP, visit, jnp.zeros((block, items_hbm.shape[2]), jnp.float32))
+        items = jnp.concatenate([vbuf[item_ref[base + i]] for i in range(per_user)], axis=0)
+        ratings = jnp.concatenate([rbuf[pos_ref[base + i]] for i in range(per_user)], axis=1)
+        predicted = lax.dot_general(
+            rows_of_user, items, (((1,), (1,)), ((), ())), preferred_element_type=jnp.float32
+        )
+        ratings = ratings.astype(jnp.float32)
+        if stage == 0:
+            weights = jnp.where(ratings != 0, ratings - predicted, 0.0)
+        else:
+            weights = jnp.where(ratings != 0, predicted, 0.0)
+        return jnp.dot(weights.astype(jnp.bfloat16), items, preferred_element_type=jnp.float32)
 
     def reduced(stage):
-        for d in list(range(1, cols)) + [0]:
+        for d in [0] + order:
             if d:
-                pltpu.make_async_remote_copy(
-                    src_ref=pbuf.at[stage, my_col],
-                    dst_ref=pbuf.at[stage, my_col],
-                    send_sem=g_send.at[stage, cols - d],
-                    recv_sem=g_recv.at[stage, cols - d],
-                    device_id={"col": col_of(cols - d)},
-                    device_id_type=MESH,
-                ).wait_recv()
+                gather_copy(stage, d).wait_recv()
             col = col_of(d)
 
             def one(j, carry):
-                part[stage, d, pl.ds(pl.multiple_of(j * block, block), block), :] = user_terms(stage, col, j)
+                part[stage, d, j] = user_terms(stage, col, j)
                 return carry
 
             lax.fori_loop(0, own_users, one, 0)
             if d:
-                scatter_copy(stage, d).start()
-        total = part[stage, 0]
-        for d in range(1, cols):
-            scatter_copy(stage, d).wait_recv()
-            total = total + recv[stage, d]
-        return total
-
-    x_ref[...] = uf_ref[...]
-    residual = reduced(0) - damp_ref[...] * uf_ref[...]
+                for j in range(own_users):
+                    bit = 1
+                    while bit < (d & -d):
+                        scatter_copy(stage, d | bit, j).wait_recv()
+                        part[stage, d, j] = part[stage, d, j] + recv[stage, d | bit, j]
+                        bit *= 2
+                    scatter_copy(stage, d, j).start()
+        totals = []
+        for j in range(own_users):
+            total = part[stage, 0, j]
+            bit = 1
+            while bit < cols:
+                scatter_copy(stage, bit, j).wait_recv()
+                total = total + recv[stage, bit, j]
+                bit *= 2
+            totals.append(total)
+        return jnp.concatenate(totals, axis=0)
+
+    residual = reduced(0) - damp_ref[...] * x_ref[...]
     r_ref[...] = residual
     p_ref[...] = residual
     squares = jnp.sum(residual * residual, axis=1, keepdims=True)
     for iteration in range(ITERS):
         pbuf[iteration + 1, my_col] = p_ref[...].astype(jnp.bfloat16)
-        for d in range(1, cols):
+        for d in order:
             gather_copy(iteration + 1, d).start()
         image = reduced(iteration + 1) + damp_ref[...] * p_ref[...]
         direction = p_ref[...]
@@ -196,7 +210,8 @@
     for stage in range(ITERS + 1):
         for d in range(1, cols):
             gather_copy(stage, d).wait_send()
-            scatter_copy(stage, d).wait_send()
+            for j in range(own_users):
+                scatter_copy(stage, d, j).wait_send()
 
 
 def per_device(sizes, slab_users, user_factors, item_factors, ratings, block_user, block_item, counts):
@@ -222,7 +237,6 @@
     match = wanted[:, None] == ranks[None, :]
     positions = jnp.sum(jnp.where(match, here[None, :], 0), axis=1)
     items = jnp.sum(jnp.where(match, columns[None, :], 0), axis=1)
-    damping = jnp.broadcast_to(reg_weight * counts.astype(jnp.float32)[:, None], (users, rank))
 
     stages = ITERS + 1
     dma = pltpu.SemaphoreType.DMA
@@ -235,15 +249,19 @@
             jax.ShapeDtypeStruct((users, rank), jnp.float32),
             jax.ShapeDtypeStruct((users, rank), jnp.float32),
         ),
-        in_specs=[smem, smem, vmem, vmem, hbm, hbm],
+        in_specs=[smem, smem, hbm, hbm, hbm, hbm],
         out_specs=(vmem, vmem),
         scratch_shapes=[
             pltpu.VMEM((rows * item_blocks, block, rank), jnp.bfloat16),
             pltpu.VMEM((fibers * held_blocks, block, block), jnp.bfloat16),
             pltpu.VMEM((stages, cols, users, rank), jnp.bfloat16),
-            pltpu.VMEM((stages, cols, users, rank), jnp.float32),
-            pltpu.VMEM((stages, cols, users, rank), jnp.float32),
+            pltpu.VMEM((stages, cols, own_users, block, rank), jnp.float32),
+            pltpu.VMEM((stages, cols, own_users, block, rank), jnp.float32),
             pltpu.VMEM((users, rank), jnp.float32),
+            pltpu.VMEM((users, rank), jnp.float32),
+            pltpu.VMEM((own_users, block), jnp.int32),
+            dma,
+            dma,
             dma,
             dma,
             dma((rows,)),
@@ -254,17 +272,17 @@
             dma((fibers,)),
             dma((stages, cols)),
             dma((stages, cols)),
-            dma((stages, cols)),
-            dma((stages, cols)),
+            dma((stages, cols, own_users)),
+            dma((stages, cols, own_users)),
         ],
         compiler_params=pltpu.CompilerParams(
-            collective_id=0, has_side_effects=True, vmem_limit_bytes=48 * 1024 * 1024
+            collective_id=0, has_side_effects=True, vmem_limit_bytes=67043328
         ),
     )(
         positions,
         items,
         user_factors,
-        damping,
+        counts.reshape(own_users, block),
         item_factors.reshape(item_blocks, block, rank),
         ratings[0, 0],
     )

time: 83.3 us -> 69.5 us (0.83)
  Pallas kernels: 72.7 us -> 61.8 us
  local copies, waits for them, and re-layouts: 5.53 us -> 3.22 us
    pallas_call x1, Pallas kernels: 72.7 us -> 61.8 us  [per_device(): pl.pallas_call(functools.partial(sweep_kernel, sizes), out_shape=(jax.Sha...]
    unnamed x8 -> x2, local copies, waits for them, and re-layouts: 5.35 us -> 3.14 us
where the time goes in v2:
time: 69.5 us; the launch traced here: 69.3 us
  Pallas kernels  61.8 us (89%)
  local copies, waits for them, and re-layouts  3.22 us (5%)
  blocking collectives  1.95 us (3%)
  other arithmetic  1.66 us (2%)
    pallas_call x1, Pallas kernels, per_device(): pl.pallas_call(functools.partial(sweep_kernel, sizes), out_shape=(jax.Sha...  61.8 us
    unnamed x2, local copies, waits for them, and re-layouts  3.14 us
    all_gather x1, blocking collectives, per_device(): lax.all_gather(jnp.stack([block_user[0, 0], block_item[0, 0]]), 'fiber',...  1.95 us

profile of v2, /device:TPU:0, one launch (start us, length us, event | category | flops | bytes accessed | tf_op | source)
XLA Modules:
  0.0 69.3 jit_solution(5148506306793989290)
XLA Ops:
  0.6 0.7 add_bitcast_fusion
  1.3 1.9 %all-gather.1 = s32[2,2,128]{2,1,0:T(2,128)S(1)} all-gather(s32[1,2,128]{2,1,0:T(2,128)S(1)} %add_bitcast_fusion), channel_id=2, replica_groups=mesh['row'=4,'col'=4,'fiber'=2] {'fiber'}, dimensions={0}, use_global_device_ids=true | all-gather | bytes 3072 | tf_op jit(solution)/shard_map/all_gather | solution.py:226
  3.3 0.2 convert_reduce_fusion
  3.5 0.1 iota_add_fusion
  3.5 0.1 add.51
  3.6 0.7 %fusion.1 = (s32[128]{0:T(128)}, s32[128]{0:T(128)}) fusion(s32[256]{0:T(256)S(1)} %bitcast.13, s32[256]{0:T(256)S(1)} %convert_reduce_fusion, s32[128]{0:T(128)S(1)} %add.51), kind=kLoop, calls=%fused_computation.4 | loop fusion | flops 163584 | bytes 3584 | tf_op jit(solution)/shard_map/reduce_sum | solution.py:239
  4.3 61.8 %shard_map.77 = (f32[256,128]{1,0:T(8,128)}, f32[256,128]{1,0:T(8,128)}) custom-call(s32[128]{0:T(128)} %get-tuple-element.3.pos_ref, s32[128]{0:T(128)} %get-tuple-element.2.item_ref, f32[256,128]{1,0:T(8,128)} %uf_hbm.1, s32[2,128]{1,0:T(2,128)} %bitcast.15, bf16[8,128,128]{2,1,0:T(8,128)(2,1)} %bitcast.12, bf16[128,128,128]{2,1,0:T(8,128)(2,1)} %bitcast.11), custom_call_target="tpu_custom_call" | custom-call | tf_op jit(solution)/shard_map/pallas_call | solution.py:246
  66.2 1.6 %copy.10 = f32[256,128]{1,0:T(8,128)} copy(f32[256,128]{1,0:T(8,128)} %get-tuple-element.8) | data formatting | bytes 262144
  67.7 1.6 %copy.11 = f32[256,128]{1,0:T(8,128)} copy(f32[256,128]{1,0:T(8,128)} %get-tuple-element.9) | data formatting | bytes 262144
  (3 shorter events, 0.0 us)

commit v3 on v2

--- a/solution.py
+++ b/solution.py
@@ -62,15 +62,16 @@
         pl.semaphore_signal(barrier, inc=1, device_id={"fiber": fiber_of(d)}, device_id_type=MESH)
 
     user_load.wait()
-    pbuf[0, my_col] = x_ref[...].astype(jnp.bfloat16)
+    for j in range(own_users):
+        pbuf[0, my_col, j] = x_ref[pl.ds(j * block, block), :].astype(jnp.bfloat16)
     pl.semaphore_wait(barrier, rows + cols + fibers - 3)
 
-    def gather_copy(stage, d):
+    def gather_copy(stage, d, j):
         return pltpu.make_async_remote_copy(
-            src_ref=pbuf.at[stage, my_col],
-            dst_ref=pbuf.at[stage, my_col],
-            send_sem=g_send.at[stage, d],
-            recv_sem=g_recv.at[stage, d],
+            src_ref=pbuf.at[stage, my_col, j],
+            dst_ref=pbuf.at[stage, my_col, j],
+            send_sem=g_send.at[stage, d, j],
+            recv_sem=g_recv.at[stage, d, j],
             device_id={"col": col_of(d)},
             device_id_type=MESH,
         )
@@ -98,8 +99,9 @@
         copy.start()
         item_sends.append(copy)
     order = sorted(range(1, cols), key=lambda d: (d & -d, -d))
-    for d in order:
-        gather_copy(0, d).start()
+    for j in range(own_users):
+        for d in order:
+            gather_copy(0, d, j).start()
     rating_sends = []
     for e in range(1, fibers):
         copy = pltpu.make_async_remote_copy(
@@ -141,7 +143,7 @@
         copy.wait_recv()
 
     def user_terms(stage, col, j):
-        rows_of_user = pbuf[stage, col, pl.ds(pl.multiple_of(j * block, block), block), :]
+        rows_of_user = pbuf[stage, col, j]
         base = (col * own_users + j) * per_user
 
         items = jnp.concatenate([vbuf[item_ref[base + i]] for i in range(per_user)], axis=0)
@@ -156,61 +158,65 @@
             weights = jnp.where(ratings != 0, predicted, 0.0)
         return jnp.dot(weights.astype(jnp.bfloat16), items, preferred_element_type=jnp.float32)
 
-    def reduced(stage):
-        for d in [0] + order:
-            if d:
-                gather_copy(stage, d).wait_recv()
-            col = col_of(d)
-
-            def one(j, carry):
-                part[stage, d, j] = user_terms(stage, col, j)
-                return carry
-
-            lax.fori_loop(0, own_users, one, 0)
-            if d:
+    def add_received(stage, d, j):
+        total = part[stage, d, j]
+        bit = 1
+        while bit < (d & -d if d else cols):
+            scatter_copy(stage, d | bit, j).wait_recv()
+            total = total + recv[stage, d | bit, j]
+            bit *= 2
+        return total
+
+    def scatter(stage):
+        for j in range(own_users):
+            for d in [0] + order:
+                if d:
+                    gather_copy(stage, d, j).wait_recv()
+                part[stage, d, j] = user_terms(stage, col_of(d), j)
+                if d & 1:
+                    scatter_copy(stage, d, j).start()
+        for d in order:
+            if d & 1 == 0:
                 for j in range(own_users):
-                    bit = 1
-                    while bit < (d & -d):
-                        scatter_copy(stage, d | bit, j).wait_recv()
-                        part[stage, d, j] = part[stage, d, j] + recv[stage, d | bit, j]
-                        bit *= 2
+                    part[stage, d, j] = add_received(stage, d, j)
                     scatter_copy(stage, d, j).start()
-        totals = []
+
+    def begin(stage, j, direction):
+        users = pl.ds(j * block, block)
+        p_ref[users, :] = direction
+        pbuf[stage, my_col, j] = direction.astype(jnp.bfloat16)
+        for d in order:
+            gather_copy(stage, d, j).start()
+
+    scatter(0)
+    squares = []
+    for j in range(own_users):
+        users = pl.ds(j * block, block)
+        residual = add_received(0, 0, j) - damp_ref[users, :] * x_ref[users, :]
+        begin(1, j, residual)
+        r_ref[users, :] = residual
+        squares.append(jnp.sum(residual * residual, axis=1, keepdims=True))
+    for iteration in range(ITERS):
+        scatter(iteration + 1)
         for j in range(own_users):
-            total = part[stage, 0, j]
-            bit = 1
-            while bit < cols:
-                scatter_copy(stage, bit, j).wait_recv()
-                total = total + recv[stage, bit, j]
-                bit *= 2
-            totals.append(total)
-        return jnp.concatenate(totals, axis=0)
-
-    residual = reduced(0) - damp_ref[...] * x_ref[...]
-    r_ref[...] = residual
-    p_ref[...] = residual
-    squares = jnp.sum(residual * residual, axis=1, keepdims=True)
-    for iteration in range(ITERS):
-        pbuf[iteration + 1, my_col] = p_ref[...].astype(jnp.bfloat16)
-        for d in order:
-            gather_copy(iteration + 1, d).start()
-        image = reduced(iteration + 1) + damp_ref[...] * p_ref[...]
-        direction = p_ref[...]
-        step_size = squares / (jnp.sum(direction * image, axis=1, keepdims=True) + tiny)
-        x_ref[...] = x_ref[...] + step_size * direction
-        residual = r_ref[...] - step_size * image
-        r_ref[...] = residual
-        if iteration + 1 < ITERS:
-            renewed = jnp.sum(residual * residual, axis=1, keepdims=True)
-            p_ref[...] = residual + renewed / (squares + tiny) * direction
-            squares = renewed
+            users = pl.ds(j * block, block)
+            direction = p_ref[users, :]
+            image = add_received(iteration + 1, 0, j) + damp_ref[users, :] * direction
+            step_size = squares[j] / (jnp.sum(direction * image, axis=1, keepdims=True) + tiny)
+            residual = r_ref[users, :] - step_size * image
+            if iteration + 1 < ITERS:
+                renewed = jnp.sum(residual * residual, axis=1, keepdims=True)
+                begin(iteration + 2, j, residual + renewed / (squares[j] + tiny) * direction)
+                squares[j] = renewed
+            r_ref[users, :] = residual
+            x_ref[users, :] = x_ref[users, :] + step_size * direction
 
     for copy in item_sends + rating_sends + shared:
         copy.wait_send()
     for stage in range(ITERS + 1):
         for d in range(1, cols):
-            gather_copy(stage, d).wait_send()
             for j in range(own_users):
+                gather_copy(stage, d, j).wait_send()
                 scatter_copy(stage, d, j).wait_send()
 
 
@@ -254,7 +260,7 @@
         scratch_shapes=[
             pltpu.VMEM((rows * item_blocks, block, rank), jnp.bfloat16),
             pltpu.VMEM((fibers * held_blocks, block, block), jnp.bfloat16),
-            pltpu.VMEM((stages, cols, users, rank), jnp.bfloat16),
+            pltpu.VMEM((stages, cols, own_users, block, rank), jnp.bfloat16),
             pltpu.VMEM((stages, cols, own_users, block, rank), jnp.float32),
             pltpu.VMEM((stages, cols, own_users, block, rank), jnp.float32),
             pltpu.VMEM((users, rank), jnp.float32),
@@ -270,8 +276,8 @@
             dma((rows, fibers)),
             dma((fibers,)),
             dma((fibers,)),
-            dma((stages, cols)),
-            dma((stages, cols)),
+            dma((stages, cols, own_users)),
+            dma((stages, cols, own_users)),
             dma((stages, cols, own_users)),
             dma((stages, cols, own_users)),
         ],

time: 69.5 us -> 68 us (0.978)
  Pallas kernels: 61.8 us -> 60.3 us
    pallas_call x1, Pallas kernels: 61.8 us -> 60.3 us  [per_device(): pl.pallas_call(functools.partial(sweep_kernel, sizes), out_shape=(jax.Sha...]
where the time goes in v3:
time: 68 us; the launch traced here: 67.8 us
  Pallas kernels  60.3 us (89%)
  local copies, waits for them, and re-layouts  3.22 us (5%)
  blocking collectives  1.95 us (3%)
  other arithmetic  1.66 us (2%)
    pallas_call x1, Pallas kernels, per_device(): pl.pallas_call(functools.partial(sweep_kernel, sizes), out_shape=(jax.Sha...  60.3 us
    unnamed x2, local copies, waits for them, and re-layouts  3.14 us
    all_gather x1, blocking collectives, per_device(): lax.all_gather(jnp.stack([block_user[0, 0], block_item[0, 0]]), 'fiber',...  1.95 us

profile of v3, /device:TPU:0, one launch (start us, length us, event | category | flops | bytes accessed | tf_op | source)
XLA Modules:
  0.0 67.8 jit_solution(14515146872938587684)
XLA Ops:
  0.6 0.7 %add_bitcast_fusion = s32[1,2,128]{2,1,0:T(2,128)S(1)} fusion(s32[1,128]{1,0:T(1,128)} %bitcast.16, s32[1,128]{1,0:T(1,128)} %bitcast.17), kind=kLoop, calls=%fused_computation.7 | loop fusion | flops 256 | bytes 2048
  1.3 1.9 %all-gather.1 = s32[2,2,128]{2,1,0:T(2,128)S(1)} all-gather(s32[1,2,128]{2,1,0:T(2,128)S(1)} %add_bitcast_fusion), channel_id=2, replica_groups=mesh['row'=4,'col'=4,'fiber'=2] {'fiber'}, dimensions={0}, use_global_device_ids=true | all-gather | bytes 3072 | tf_op jit(solution)/shard_map/all_gather | solution.py:232
  3.3 0.2 convert_reduce_fusion
  3.5 0.1 iota_add_fusion
  3.5 0.1 add.51
  3.6 0.7 %fusion.1 = (s32[128]{0:T(128)}, s32[128]{0:T(128)}) fusion(s32[256]{0:T(256)S(1)} %bitcast.13, s32[256]{0:T(256)S(1)} %convert_reduce_fusion, s32[128]{0:T(128)S(1)} %add.51), kind=kLoop, calls=%fused_computation.4 | loop fusion | flops 163584 | bytes 3584 | tf_op jit(solution)/shard_map/reduce_sum | solution.py:245
  4.3 60.3 %shard_map.77 = (f32[256,128]{1,0:T(8,128)}, f32[256,128]{1,0:T(8,128)}) custom-call(s32[128]{0:T(128)} %get-tuple-element.3.pos_ref, s32[128]{0:T(128)} %get-tuple-element.2.item_ref, f32[256,128]{1,0:T(8,128)} %uf_hbm.1, s32[2,128]{1,0:T(2,128)} %bitcast.15, bf16[8,128,128]{2,1,0:T(8,128)(2,1)} %bitcast.12, bf16[128,128,128]{2,1,0:T(8,128)(2,1)} %bitcast.11), custom_call_target="tpu_custom_call" | custom-call | tf_op jit(solution)/shard_map/pallas_call | solution.py:252
  64.6 1.6 %copy.10 = f32[256,128]{1,0:T(8,128)} copy(f32[256,128]{1,0:T(8,128)} %get-tuple-element.8) | data formatting | bytes 262144
  66.2 1.6 %copy.11 = f32[256,128]{1,0:T(8,128)} copy(f32[256,128]{1,0:T(8,128)} %get-tuple-element.9) | data formatting | bytes 262144
  (3 shorter events, 0.0 us)
